TPU v7x, 256 devices: a whole 4x4x8 slice. The times are simulated.
256 devices in a mesh: bead: 16 (over x, z_hi), space: 16 (over z_lo, y, core).
Axes of the slice: x: 4, y: 4, z: 8 (z_hi: 4, z_lo: 2; z = z_hi * 2 + z_lo), core: 2. Of those that a mesh axis runs over, the one named last changes fastest.
Arguments:
- positions: float32 [64, 3, 4096], P('bead', None, 'space'), may hold values from -1 to 17
- species: int32 [4096], P('space'), may hold values from 0 to 1
- neighbors: int32 [32, 4096], P(None, 'space'), may hold values from 0 to 383, as said below
- counts: int32 [4096], P('space'), may hold values from 1 to 32, as said below
- send_rows: int32 [2048], P('space'), may hold values from 0 to 255, as said below
- embed: float32 [2, 128], replicated, may hold values from -6 to 6
- w_radial: float32 [2, 8, 128], replicated, may hold values from -2 to 2
- w_msg: float32 [2, 128, 128], replicated, may hold values from -0.5 to 0.5
- w_upd: float32 [2, 128, 128], replicated, may hold values from -0.5 to 0.5
- w_out: float32 [128], replicated, may hold values from -0.5 to 0.5
Outputs:
- forces: float32 [64, 3, 4096], P('bead', None, 'space')
Inputs may be any that keep to these rules, and one draw needn't show every extreme that they name: `neighbors`: entry n < 256 is the domain's own row n; 256 + s is the s-th left ghost and 320 + s the s-th right ghost. `counts`: slots of an atom below its count are live, the others padding. `send_rows`: each domain's first 64 entries are a permutation of its rows 0 to 63, the next 64 a permutation of its rows 192 to 255.
All inputs are finite; a program needn't handle non-finite values.
Results may differ from a plain program's by a relative error of at most 0.0003.
Values sent between devices are 32-bit elements; how exact they have to be, the bound alone decides.
A program may use at most 64 MiB of HBM per device.

v0:
```python
from functools import partial
import jax
import jax.numpy as jnp
from jax import lax
from jax.sharding import PartitionSpec as P

PC = 16
exact_mode = lax.Precision.HIGHEST
spacing_floor = 0.01
radial_width = 0.2
radial_reach = 1.5
block_rows = 128


def with_halo(block, sides, width):
    for axis, dim in sides:
        count = lax.axis_size(axis)
        forward = [(i, i + 1) for i in range(count - 1)]
        forward.append((count - 1, 0))
        backward = [(target, source) for source, target in forward]
        low = lax.ppermute(
            lax.slice_in_dim(block, block.shape[dim] - width, None, axis=dim), axis, forward
        )
        high = lax.ppermute(lax.slice_in_dim(block, 0, width, axis=dim), axis, backward)
        block = jnp.concatenate([low, block, high], axis=dim)
    return block


def contraction(full_beads, reduced_beads):
    rowpos = jnp.arange(reduced_beads, dtype=jnp.float32)[:, None]
    colpos = jnp.arange(full_beads, dtype=jnp.float32)[None, :]
    phase_gap = rowpos / reduced_beads - colpos / full_beads
    running = jnp.ones_like(phase_gap)
    for harmonic in range(1, reduced_beads // 2):
        running = running + 2.0 * jnp.cos(2.0 * jnp.pi * harmonic * phase_gap)
    running = running + jnp.cos(jnp.pi * reduced_beads * phase_gap)
    return running / full_beads


def silu_slope(argument):
    sigmoid_part = jax.nn.sigmoid(argument)
    return sigmoid_part * (1.0 + argument * (1.0 - sigmoid_part))


def blocked(values, which_axis):
    dims_now = values.shape
    blocks = dims_now[which_axis] // block_rows
    reshaped = values.reshape(
        dims_now[:which_axis] + (blocks, block_rows) + dims_now[which_axis + 1 :]
    )
    return jnp.moveaxis(reshaped, which_axis, 0)


def unblocked(values, which_axis):
    moved_axes = jnp.moveaxis(values, 0, which_axis)
    dims_now = moved_axes.shape
    merged = (dims_now[which_axis] * dims_now[which_axis + 1],)
    return moved_axes.reshape(dims_now[:which_axis] + merged + dims_now[which_axis + 2 :])


def chooser_table(rows, extent):
    columns = lax.broadcasted_iota(jnp.int32, rows.shape + (extent,), rows.ndim)
    return (rows[..., None] == columns).astype(jnp.float32)


def block_message(lent_ext, radial_basis, live_slots, neighbor_rows, radial_map, edge_scale):
    radial_w = jnp.einsum("nbkr,nc->bkrc", radial_basis, radial_map, precision=exact_mode)
    chooser = chooser_table(neighbor_rows, lent_ext.shape[1])
    near_rows = jnp.einsum("kre,bec->bkrc", chooser, lent_ext, precision=exact_mode)
    return edge_scale * jnp.einsum(
        "bkrc,kr->brc", radial_w * near_rows, live_slots, precision=exact_mode
    )


def block_backward(state_pair, inputs, lent_ext, radial_map, edge_scale, want_features):
    grad_lent, grad_points = state_pair
    radial_basis, offsets, displace, distance, live_slots, neighbor_rows, grad_message = inputs
    radial_w = jnp.einsum("nbkr,nc->bkrc", radial_basis, radial_map, precision=exact_mode)
    chooser = chooser_table(neighbor_rows, lent_ext.shape[1])
    near_rows = jnp.einsum("kre,bec->bkrc", chooser, lent_ext, precision=exact_mode)
    weighted = edge_scale * live_slots[None, :, :, None] * grad_message[:, None]
    grad_radial = weighted * near_rows
    grad_basis = jnp.einsum("bkrc,nc->nbkr", grad_radial, radial_map, precision=exact_mode)
    grad_distance = jnp.sum(grad_basis * radial_basis * offsets, axis=0) * (-2.0 / radial_width)
    grad_displace = grad_distance[:, None] * displace / distance[:, None]
    grad_points = grad_points + jnp.einsum(
        "kre,bckr->bce", chooser, grad_displace, precision=exact_mode
    )
    if want_features:
        grad_near = weighted * radial_w
        grad_lent = grad_lent + jnp.einsum(
            "kre,bkrc->bec", chooser, grad_near, precision=exact_mode
        )
    return ((grad_lent, grad_points), -jnp.sum(grad_displace, axis=2))


def on_device(
    positions, species, neighbors, counts, send_rows, embed, w_radial, w_msg, w_upd, w_out
):
    full_dev = positions.shape[0]
    atom_count = positions.shape[2]
    beads_all = full_dev * lax.axis_size("bead")
    reduced_dev = PC // lax.axis_size("bead")
    bead_index = lax.axis_index("bead")
    contract_table = contraction(beads_all, PC)
    own_columns = lax.dynamic_slice_in_dim(contract_table, bead_index * full_dev, full_dev, 1)
    own_table = lax.dynamic_slice_in_dim(contract_table, bead_index * reduced_dev, reduced_dev, 0)
    weights = own_table
    reduced = jnp.einsum(
        "kj,jcn->kcn",
        weights,
        lax.all_gather(positions, "bead", axis=0, tiled=True),
        precision=exact_mode,
    )
    ghost_count = send_rows.shape[0] // 2
    domains = lax.axis_size("space")
    domain = lax.axis_index("space")
    selector = chooser_table(send_rows, atom_count)
    lent_points = jnp.einsum("ga,bca->bcg", selector, reduced, precision=exact_mode)
    lent_species = jnp.dot(selector, species.astype(jnp.float32), precision=exact_mode)
    lent_species = lent_species[None, None]
    outgoing = jnp.concatenate([lent_points, lent_species], axis=1)
    arrived = with_halo(outgoing, (("space", 2),), ghost_count)
    borrowed = jnp.concatenate(
        [arrived[:, :, :ghost_count], arrived[:, :, 3 * ghost_count :]], axis=2
    )
    left_shift = jnp.where(domain == 0, -float(domains), 0.0)
    right_shift = jnp.where(domain == domains - 1, float(domains), 0.0)
    ghost_slot = jnp.arange(2 * ghost_count, dtype=jnp.int32)
    box_shift = jnp.where(ghost_slot < ghost_count, left_shift, right_shift).astype(jnp.float32)
    ghost_points = borrowed[:, :3].at[:, 0].add(box_shift[None])
    ghost_species = borrowed[0, 3]
    ext_points = jnp.concatenate([reduced, ghost_points], axis=2)
    extent = ext_points.shape[2]
    blocks_rows = blocked(neighbors, 1)

    def pick_points(rows_block):
        chooser = chooser_table(rows_block, extent)
        return jnp.einsum("kre,bce->bckr", chooser, ext_points, precision=exact_mode)

    near_points = unblocked(lax.map(pick_points, blocks_rows), 3)
    displace = near_points - reduced[:, :, None, :]
    distance = jnp.sqrt(jnp.sum(displace * displace, axis=1) + spacing_floor)
    basis_count = w_radial.shape[1]
    centers = radial_reach * jnp.arange(basis_count, dtype=jnp.float32) / (basis_count - 1)
    offsets = (distance[None] - centers[:, None, None, None]) / radial_width
    radial_basis = jnp.exp(-offsets * offsets)
    slot_index = lax.broadcasted_iota(jnp.int32, neighbors.shape, 0)
    live_slots = (slot_index < counts[None, :]).astype(jnp.float32)
    edge_scale = neighbors.shape[0] ** (-0.5)
    kinds = jnp.arange(embed.shape[0], dtype=jnp.int32)
    own_onehot = (species[:, None] == kinds[None, :]).astype(jnp.float32)
    ghost_onehot = (ghost_species[:, None] == kinds.astype(jnp.float32)[None, :]).astype(
        jnp.float32
    )
    ext_onehot = jnp.concatenate([own_onehot, ghost_onehot], axis=0)
    hidden = jnp.dot(own_onehot, embed, precision=exact_mode)[None]
    first_table = jnp.dot(embed, w_msg[0], precision=exact_mode)
    blocks_basis = blocked(radial_basis, 3)
    blocks_offsets = blocked(offsets, 3)
    blocks_displace = blocked(displace, 3)
    blocks_distance = blocked(distance, 2)
    blocks_live = blocked(live_slots, 1)
    layer_total = w_msg.shape[0]
    saved = []
    for layer_index in range(layer_total):
        if layer_index == 0:
            first_rows = jnp.dot(ext_onehot, first_table, precision=exact_mode)
            lent_ext = first_rows[None]
        else:
            lent_own = jnp.einsum("bac,cd->bad", hidden, w_msg[layer_index], precision=exact_mode)
            outgoing_rows = jnp.einsum("ga,bac->bgc", selector, lent_own, precision=exact_mode)
            arrived_rows = with_halo(outgoing_rows, (("space", 1),), ghost_count)
            lent_ext = jnp.concatenate(
                [lent_own, arrived_rows[:, :ghost_count], arrived_rows[:, 3 * ghost_count :]],
                axis=1,
            )
        radial_map = w_radial[layer_index]
        per_block = lax.map(
            lambda parts: block_message(
                lent_ext, parts[0], parts[1], parts[2], radial_map, edge_scale
            ),
            (blocks_basis, blocks_live, blocks_rows),
        )
        message = unblocked(per_block, 1)
        update = jnp.einsum("bac,cd->bad", message, w_upd[layer_index], precision=exact_mode)
        saved.append((lent_ext, update))
        hidden = hidden + jax.nn.silu(update)
    grad_hidden = jnp.broadcast_to(w_out[None, None], hidden.shape)
    grad_points = jnp.zeros(ext_points.shape, jnp.float32)
    center_pull = jnp.zeros(reduced.shape, jnp.float32)
    for layer_index in reversed(range(layer_total)):
        lent_ext, update = saved[layer_index]
        grad_update = grad_hidden * silu_slope(update)
        grad_message = jnp.einsum(
            "bac,dc->bad", grad_update, w_upd[layer_index], precision=exact_mode
        )
        want_features = layer_index > 0
        if want_features:
            start_lent = jnp.zeros(lent_ext.shape, jnp.float32)
        else:
            start_lent = jnp.zeros((1,), jnp.float32)
        step_function = partial(
            block_backward,
            lent_ext=lent_ext,
            radial_map=w_radial[layer_index],
            edge_scale=edge_scale,
            want_features=want_features,
        )
        scanned = (
            blocks_basis,
            blocks_offsets,
            blocks_displace,
            blocks_distance,
            blocks_live,
            blocks_rows,
            blocked(grad_message, 1),
        )
        (grad_lent, grad_points), pulls = lax.scan(
            step_function, (start_lent, grad_points), scanned
        )
        center_pull = center_pull + unblocked(pulls, 2)
        if want_features:
            sent_back = with_halo(grad_lent[:, atom_count:], (("space", 1),), ghost_count)
            returned = jnp.concatenate(
                [sent_back[:, :ghost_count], sent_back[:, 3 * ghost_count :]], axis=1
            )
            grad_own = grad_lent[:, :atom_count] + jnp.einsum(
                "ga,bgc->bac", selector, returned, precision=exact_mode
            )
            grad_hidden = grad_hidden + jnp.einsum(
                "bac,dc->bad", grad_own, w_msg[layer_index], precision=exact_mode
            )
    sent_force = with_halo(grad_points[:, :, atom_count:], (("space", 2),), ghost_count)
    returned_force = jnp.concatenate(
        [sent_force[:, :, :ghost_count], sent_force[:, :, 3 * ghost_count :]], axis=2
    )
    energy_grad = (
        grad_points[:, :, :atom_count]
        + center_pull
        + jnp.einsum("ga,bcg->bca", selector, returned_force, precision=exact_mode)
    )
    pull_reduced = -energy_grad
    ratio = float(beads_all) / PC
    weights = own_columns
    return ratio * jnp.einsum(
        "kj,kcn->jcn",
        weights,
        lax.all_gather(pull_reduced, "bead", axis=0, tiled=True),
        precision=exact_mode,
    )


def solution(mesh):
    return jax.shard_map(
        on_device,
        mesh=mesh,
        in_specs=(
            P("bead", None, "space"),
            P("space"),
            P(None, "space"),
            P("space"),
            P("space"),
            P(),
            P(),
            P(),
            P(),
            P(),
        ),
        out_specs=P("bead", None, "space"),
        check_vma=False,
    )
```

profile of v0, /device:TPU:64, one launch (start us, length us, event | category | flops | bytes accessed | tf_op | source)
XLA Modules:
  0.0 223.0 jit_solution(11656162681923624815)
XLA Ops:
  0.7 42.8 %all_gather.6 = f32[64,3,256]{2,1,0:T(4,128)S(1)} all-gather(f32[4,3,256]{2,1,0:T(4,128)S(1)} %copy.41), channel_id=1, replica_groups=mesh['bead'=16,'space'=16] {'bead'}, dimensions={0}, use_global_device_ids=true | all-gather | bytes 208896 | tf_op jit(solution)/shard_map/all_gather | solution.py:112
  46.7 3.8 %collective-permute-start.1 = (f32[1,4,64]{2,1,0:T(4,128)S(1)}, f32[1,4,64]{2,1,0:T(4,128)S(1)}, u32[]{:S(2)}, u32[]{:S(2)}) collective-permute-start(f32[1,4,64]{2,1,0:T(4,128)S(1)} %get-tuple-element.553), channel_id=1, source_target_pairs={{1,0},{2,1},{3,2},{4,3},{5,4},{6,5},{7,6},{8,7},{9,8},{10,9},{11,1... | collective-permute-start | bytes 3080 | tf_op jit(solution)/shard_map/ppermute | solution.py:24
  54.9 7.0 %while.58 = (s32[]{:T(128)}, f32[2,1,3,32,128]{4,2,3,1,0:T(4,128)S(1)}, s32[2,32,128]{2,1,0:T(8,128)S(1)}, f32[1,3,384]{2,1,0:T(4,128)S(1)}, s32[]{:T(128)}) while((s32[]{:T(128)}, f32[2,1,3,32,128]{4,2,3,1,0:T(4,128)S(1)}, s32[2,32,128]{2,1,0:T(8,128)S(1)}, f32[1,3,384]{2,1,0:T(4,128)S(1)}, s32[]{:T(128)}) %tuple.106), condition=%wide.region_1.2_spmd, body=%wide.region_0.1_spmd.sunk | while | flops 58195968 | bytes 120901 | solution.py:141
  54.9 3.5 %fusion.252 = f32[2,1,3,32,128]{4,2,3,1,0:T(4,128)S(1)} fusion(f32[2,1,3,32,128]{4,2,3,1,0:T(4,128)S(1)} %get-tuple-element.823, s32[]{:T(128)} %get-tuple-element.822, s32[32,128]{1,0:T(8,128)S(1)} %dynamic-slice_bitcast_fusion.22, f32[1,3,384]{2,1,0:T(4,128)S(1)} %get-tuple-element.830), kind=kOutput, calls=%fused_computation.4.clone.1 | convolution fusion | flops 58195968 | bytes 88068 | tf_op jit(solution)/shard_map/while/body/eval_jaxpr/kre,bce->bckr/dot_general | solution.py:139
  58.4 3.5 %fusion.252 = f32[2,1,3,32,128]{4,2,3,1,0:T(4,128)S(1)} fusion(f32[2,1,3,32,128]{4,2,3,1,0:T(4,128)S(1)} %get-tuple-element.823, s32[]{:T(128)} %get-tuple-element.822, s32[32,128]{1,0:T(8,128)S(1)} %dynamic-slice_bitcast_fusion.22, f32[1,3,384]{2,1,0:T(4,128)S(1)} %get-tuple-element.830), kind=kOutput, calls=%fused_computation.4.clone.1 | convolution fusion | flops 58195968 | bytes 88068 | tf_op jit(solution)/shard_map/while/body/eval_jaxpr/kre,bce->bckr/dot_general | solution.py:139
  62.7 19.7 %while.59 = (s32[]{:T(128)}, f32[2,1,128,128]{3,2,1,0:T(8,128)S(1)}, f32[2,32,128]{2,1,0:T(8,128)S(1)}, f32[2,8,1,32,128]{4,1,3,2,0:T(8,128)S(1)}, f32[8,128]{1,...) while((s32[]{:T(128)}, f32[2,1,128,128]{3,2,1,0:T(8,128)S(1)}, ...), condition=%wide.region_4.5_spmd, body=%wide.region_3.4_spmd.sunk | while | flops 2474655744 | bytes 9048165 | solution.py:179
  62.7 3.4 %fusion.258 = f32[32,128,128]{2,1,0:T(8,128)S(1)} fusion(f32[2,8,1,32,128]{4,1,3,2,0:T(8,128)S(1)} %get-tuple-element.851, s32[]{:T(128)} %get-tuple-element.840, f32[8,128]{1,0:T(8,128)S(1)} %get-tuple-element.852), kind=kOutput, calls=%fused_computation.15.clone.1 | convolution fusion | flops 50331648 | bytes 2232324 | tf_op jit(solution)/shard_map/while/body/eval_jaxpr/nbkr,nc->bkrc/dot_general | solution.py:67
  66.1 3.3 %fusion.259 = f32[32,128,128]{2,1,0:T(8,128)S(1)} fusion(f32[32,128,128]{2,1,0:T(8,128)S(1)} %fusion.258, s32[32,128]{1,0:T(8,128)S(1)} %dynamic-slice_bitcast_fusion.24, f32[1,384,128]{2,1,0:T(8,128)S(1)} %get-tuple-element.854), kind=kOutput, calls=%fused_computation.11.clone.1 | convolution fusion | flops 2418016256 | bytes 4407296 | tf_op jit(solution)/shard_map/while/body/eval_jaxpr/kre,bec->bkrc/dot_general | solution.py:69
  69.6 2.9 %fusion.260 = f32[128,1,128]{2,1,0:T(1,128)S(1)} fusion(f32[32,128,1]{0,2,1:T(1,128)S(1)} %copy.85, f32[32,128,128]{2,1,0:T(8,128)S(1)} %fusion.259), kind=kOutput, calls=%fused_computation.12.clone.1 | convolution fusion | flops 6291456 | bytes 2179072 | tf_op jit(solution)/shard_map/while/body/eval_jaxpr/bkrc,kr->brc/dot_general | solution.py:70
  72.5 3.4 %fusion.258 = f32[32,128,128]{2,1,0:T(8,128)S(1)} fusion(f32[2,8,1,32,128]{4,1,3,2,0:T(8,128)S(1)} %get-tuple-element.851, s32[]{:T(128)} %get-tuple-element.840, f32[8,128]{1,0:T(8,128)S(1)} %get-tuple-element.852), kind=kOutput, calls=%fused_computation.15.clone.1 | convolution fusion | flops 50331648 | bytes 2232324 | tf_op jit(solution)/shard_map/while/body/eval_jaxpr/nbkr,nc->bkrc/dot_general | solution.py:67
  76.0 3.3 %fusion.259 = f32[32,128,128]{2,1,0:T(8,128)S(1)} fusion(f32[32,128,128]{2,1,0:T(8,128)S(1)} %fusion.258, s32[32,128]{1,0:T(8,128)S(1)} %dynamic-slice_bitcast_fusion.24, f32[1,384,128]{2,1,0:T(8,128)S(1)} %get-tuple-element.854), kind=kOutput, calls=%fused_computation.11.clone.1 | convolution fusion | flops 2418016256 | bytes 4407296 | tf_op jit(solution)/shard_map/while/body/eval_jaxpr/kre,bec->bkrc/dot_general | solution.py:69
  79.4 2.9 %fusion.260 = f32[128,1,128]{2,1,0:T(1,128)S(1)} fusion(f32[32,128,1]{0,2,1:T(1,128)S(1)} %copy.85, f32[32,128,128]{2,1,0:T(8,128)S(1)} %fusion.259), kind=kOutput, calls=%fused_computation.12.clone.1 | convolution fusion | flops 6291456 | bytes 2179072 | tf_op jit(solution)/shard_map/while/body/eval_jaxpr/bkrc,kr->brc/dot_general | solution.py:70
  83.6 1.1 fusion.133
  85.1 4.3 %collective-permute-start.3 = (f32[1,64,128]{2,1,0:T(8,128)S(1)}, f32[1,64,128]{2,1,0:T(8,128)S(1)}, u32[]{:S(2)}, u32[]{:S(2)}) collective-permute-start(f32[1,64,128]{2,1,0:T(8,128)S(1)} %get-tuple-element.538), channel_id=1, source_target_pairs={{1,0},{2,1},{3,2},{4,3},{5,4},{6,5},{7,6},{8,7},{9,8},{10,9},{11,1... | collective-permute-start | bytes 98312 | tf_op jit(solution)/shard_map/ppermute | solution.py:24
  91.7 20.9 %while.60 = (s32[]{:T(128)}, f32[2,1,128,128]{3,2,1,0:T(8,128)}, f32[2,32,128]{2,1,0:T(8,128)S(1)}, f32[2,8,1,32,128]{4,1,3,2,0:T(8,128)S(1)}, f32[8,128]{1,0:T(...) while((s32[]{:T(128)}, f32[2,1,128,128]{3,2,1,0:T(8,128)}, ...), condition=%wide.region_6.7_spmd, body=%wide.region_5.6_spmd.sunk | while | flops 2474655744 | bytes 9048673 | solution.py:179
  91.7 3.4 %fusion.266 = f32[32,128,128]{2,1,0:T(8,128)S(1)} fusion(f32[2,8,1,32,128]{4,1,3,2,0:T(8,128)S(1)} %get-tuple-element.875, s32[]{:T(128)} %get-tuple-element.864, f32[8,128]{1,0:T(8,128)S(1)} %get-tuple-element.876), kind=kOutput, calls=%fused_computation.31.clone.1 | convolution fusion | flops 50331648 | bytes 2232324 | tf_op jit(solution)/shard_map/while/body/eval_jaxpr/nbkr,nc->bkrc/dot_general | solution.py:67
  95.2 3.3 %fusion.267 = f32[32,128,128]{2,1,0:T(8,128)S(1)} fusion(f32[32,128,128]{2,1,0:T(8,128)S(1)} %fusion.266, s32[32,128]{1,0:T(8,128)S(1)} %dynamic-slice_bitcast_fusion.26, f32[1,384,128]{2,1,0:T(8,128)S(1)} %get-tuple-element.878), kind=kOutput, calls=%fused_computation.27.clone.1 | convolution fusion | flops 2418016256 | bytes 4407296 | tf_op jit(solution)/shard_map/while/body/eval_jaxpr/kre,bec->bkrc/dot_general | solution.py:69
  98.6 2.9 %fusion.268 = f32[128,1,128]{2,1,0:T(1,128)S(1)} fusion(f32[32,128,1]{0,2,1:T(1,128)S(1)} %copy.87, f32[32,128,128]{2,1,0:T(8,128)S(1)} %fusion.267), kind=kOutput, calls=%fused_computation.28.clone.1 | convolution fusion | flops 6291456 | bytes 2179072 | tf_op jit(solution)/shard_map/while/body/eval_jaxpr/bkrc,kr->brc/dot_general | solution.py:70
  102.2 3.4 %fusion.266 = f32[32,128,128]{2,1,0:T(8,128)S(1)} fusion(f32[2,8,1,32,128]{4,1,3,2,0:T(8,128)S(1)} %get-tuple-element.875, s32[]{:T(128)} %get-tuple-element.864, f32[8,128]{1,0:T(8,128)S(1)} %get-tuple-element.876), kind=kOutput, calls=%fused_computation.31.clone.1 | convolution fusion | flops 50331648 | bytes 2232324 | tf_op jit(solution)/shard_map/while/body/eval_jaxpr/nbkr,nc->bkrc/dot_general | solution.py:67
  105.6 3.3 %fusion.267 = f32[32,128,128]{2,1,0:T(8,128)S(1)} fusion(f32[32,128,128]{2,1,0:T(8,128)S(1)} %fusion.266, s32[32,128]{1,0:T(8,128)S(1)} %dynamic-slice_bitcast_fusion.26, f32[1,384,128]{2,1,0:T(8,128)S(1)} %get-tuple-element.878), kind=kOutput, calls=%fused_computation.27.clone.1 | convolution fusion | flops 2418016256 | bytes 4407296 | tf_op jit(solution)/shard_map/while/body/eval_jaxpr/kre,bec->bkrc/dot_general | solution.py:69
  109.1 2.9 %fusion.268 = f32[128,1,128]{2,1,0:T(1,128)S(1)} fusion(f32[32,128,1]{0,2,1:T(1,128)S(1)} %copy.87, f32[32,128,128]{2,1,0:T(8,128)S(1)} %fusion.267), kind=kOutput, calls=%fused_computation.28.clone.1 | convolution fusion | flops 6291456 | bytes 2179072 | tf_op jit(solution)/shard_map/while/body/eval_jaxpr/bkrc,kr->brc/dot_general | solution.py:70
  112.6 1.2 multiply_multiply_fusion
  114.1 32.4 %while.62 = (s32[]{:T(128)}, f32[1,384,128]{1,2,0:T(8,128)}, f32[1,3,384]{2,1,0:T(4,128)S(1)}, f32[2,1,3,128]{3,2,1,0:T(4,128)S(1)}, f32[2,32,128]{2,1,0:T(8,128...) while((s32[]{:T(128)}, f32[1,384,128]{1,2,0:T(8,128)}, ...), condition=%wide.region_10.11_spmd.clone, body=%wide.region_7.10_spmd.clone.sunk | while | flops 4996204544 | bytes 10068156 | solution.py:219
  114.3 3.4 %fusion.284 = f32[32,128,128]{2,1,0:T(8,128)S(1)} fusion(f32[2,8,1,32,128]{4,1,3,2,0:T(8,128)S(1)} %get-tuple-element.916, s32[]{:T(128)} %get-tuple-element.895, f32[8,128]{1,0:T(8,128)S(1)} %get-tuple-element.917), kind=kOutput, calls=%fused_computation.99.clone.1 | convolution fusion | flops 50331648 | bytes 2232324 | tf_op jit(solution)/shard_map/while/body/eval_jaxpr/nbkr,nc->bkrc/dot_general | solution.py:78
  117.8 4.2 %fusion.285 = f32[1,384,128]{1,2,0:T(8,128)} fusion(s32[32,128]{1,0:T(8,128)S(1)} %dynamic-slice_bitcast_fusion.30, f32[32,128,128]{2,1,0:T(8,128)S(1)} %fusion.284, f32[128,128]{1,0:T(8,128)S(1)} %dynamic-slice_bitcast_fusion.31, f32[32,128]{1,0:T(8,128)S(1)} %multiply_bitcast_fusion.5, f32[1,384,128]{1,2,0:T(8,128)} %get-tuple-element.896, ...), kind=kOutput, calls=%fused_computation.87.clone.1 | convolution fusion | flops 2418638848 | bytes 2588673 | tf_op jit(solution)/shard_map/while/body/eval_jaxpr/kre,bkrc->bec/dot_general | solution.py:91
  122.0 3.2 %fusion.286 = f32[32,128,128]{2,1,0:T(8,128)S(1)} fusion(s32[32,128]{1,0:T(8,128)S(1)} %dynamic-slice_bitcast_fusion.30, f32[1,384,128]{2,1,0:T(8,128)S(1)} %get-tuple-element.919), kind=kOutput, calls=%fused_computation.75.clone.1 | convolution fusion | flops 2417491968 | bytes 2310144 | tf_op jit(solution)/shard_map/while/body/eval_jaxpr/kre,bec->bkrc/dot_general | solution.py:80
  125.2 2.4 %fusion.287 = f32[32,128]{1,0:T(8,128)S(1)} fusion(f32[32,128,128]{2,1,0:T(8,128)S(1)} %fusion.286, f32[128,128]{1,0:T(8,128)S(1)} %dynamic-slice_bitcast_fusion.31, f32[32,128]{1,0:T(8,128)S(1)} %multiply_bitcast_fusion.5, f32[2,8,1,32,128]{4,1,3,2,0:T(8,128)S(1)} %get-tuple-element.920, s32[]{:T(128)} %get-tuple-element.895, ...), kind=kOutput, calls=%fused_computation.91.clone.1 | convolution fusion | flops 51474432 | bytes 2461700 | tf_op jit(solution)/shard_map/while/body/eval_jaxpr/bkrc,nc->nbkr/dot_general | solution.py:83
  127.6 2.2 fusion.288
  129.9 3.4 %fusion.284 = f32[32,128,128]{2,1,0:T(8,128)S(1)} fusion(f32[2,8,1,32,128]{4,1,3,2,0:T(8,128)S(1)} %get-tuple-element.916, s32[]{:T(128)} %get-tuple-element.895, f32[8,128]{1,0:T(8,128)S(1)} %get-tuple-element.917), kind=kOutput, calls=%fused_computation.99.clone.1 | convolution fusion | flops 50331648 | bytes 2232324 | tf_op jit(solution)/shard_map/while/body/eval_jaxpr/nbkr,nc->bkrc/dot_general | solution.py:78
  133.5 5.1 %fusion.285 = f32[1,384,128]{1,2,0:T(8,128)} fusion(s32[32,128]{1,0:T(8,128)S(1)} %dynamic-slice_bitcast_fusion.30, f32[32,128,128]{2,1,0:T(8,128)S(1)} %fusion.284, f32[128,128]{1,0:T(8,128)S(1)} %dynamic-slice_bitcast_fusion.31, f32[32,128]{1,0:T(8,128)S(1)} %multiply_bitcast_fusion.5, f32[1,384,128]{1,2,0:T(8,128)} %get-tuple-element.896, ...), kind=kOutput, calls=%fused_computation.87.clone.1 | convolution fusion | flops 2418638848 | bytes 2588673 | tf_op jit(solution)/shard_map/while/body/eval_jaxpr/kre,bkrc->bec/dot_general | solution.py:91
  138.6 3.2 %fusion.286 = f32[32,128,128]{2,1,0:T(8,128)S(1)} fusion(s32[32,128]{1,0:T(8,128)S(1)} %dynamic-slice_bitcast_fusion.30, f32[1,384,128]{2,1,0:T(8,128)S(1)} %get-tuple-element.919), kind=kOutput, calls=%fused_computation.75.clone.1 | convolution fusion | flops 2417491968 | bytes 2310144 | tf_op jit(solution)/shard_map/while/body/eval_jaxpr/kre,bec->bkrc/dot_general | solution.py:80
  141.8 2.4 %fusion.287 = f32[32,128]{1,0:T(8,128)S(1)} fusion(f32[32,128,128]{2,1,0:T(8,128)S(1)} %fusion.286, f32[128,128]{1,0:T(8,128)S(1)} %dynamic-slice_bitcast_fusion.31, f32[32,128]{1,0:T(8,128)S(1)} %multiply_bitcast_fusion.5, f32[2,8,1,32,128]{4,1,3,2,0:T(8,128)S(1)} %get-tuple-element.920, s32[]{:T(128)} %get-tuple-element.895, ...), kind=kOutput, calls=%fused_computation.91.clone.1 | convolution fusion | flops 51474432 | bytes 2461700 | tf_op jit(solution)/shard_map/while/body/eval_jaxpr/bkrc,nc->nbkr/dot_general | solution.py:83
  144.2 2.2 fusion.288
  147.8 3.9 %collective-permute-start.5 = (f32[1,64,128]{1,2,0:T(8,128)S(1)}, f32[1,64,128]{1,2,0:T(8,128)S(1)}, u32[]{:S(2)}, u32[]{:S(2)}) collective-permute-start(f32[1,64,128]{1,2,0:T(8,128)S(1)} %get-tuple-element.536), channel_id=1, source_target_pairs={{1,0},{2,1},{3,2},{4,3},{5,4},{6,5},{7,6},{8,7},{9,8},{10,9},{11,1... | collective-permute-start | bytes 98312 | tf_op jit(solution)/shard_map/ppermute | solution.py:24
  151.7 1.9 collective-permute-done.4
  153.6 1.2 fusion.114
  154.8 1.3 fusion.112
  156.2 1.1 convolution_bitcast_fusion.1
  157.3 16.0 %while.61 = (s32[]{:T(128)}, f32[1,3,384]{2,1,0:T(4,128)S(1)}, f32[2,1,3,128]{3,2,1,0:T(4,128)S(1)}, f32[2,32,128]{2,1,0:T(8,128)S(1)}, f32[2,1,128,128]{3,2,1,0...) while((s32[]{:T(128)}, f32[1,3,384]{2,1,0:T(4,128)S(1)}, ...), condition=%wide.region_14.15_spmd, body=%wide.region_11.14_spmd.sunk | while | flops 2527233024 | bytes 5247133 | solution.py:219
  157.3 3.3 %fusion.273 = f32[32,128,128]{2,1,0:T(8,128)S(1)} fusion(s32[32,128]{1,0:T(8,128)S(1)} %dynamic-slice_bitcast_fusion.27, f32[1,384,128]{2,1,0:T(8,128)S(1)} %get-tuple-element.957), kind=kOutput, calls=%fused_computation.41.clone.1 | convolution fusion | flops 2417491968 | bytes 2310144 | tf_op jit(solution)/shard_map/while/body/eval_jaxpr/kre,bec->bkrc/dot_general | solution.py:80
  160.6 2.3 %fusion.274 = f32[32,128]{1,0:T(8,128)S(1)} fusion(f32[32,128,128]{2,1,0:T(8,128)S(1)} %fusion.273, f32[128,128]{1,0:T(8,128)S(1)} %dynamic-slice_bitcast_fusion.29, f32[32,128]{1,0:T(8,128)S(1)} %multiply_bitcast_fusion.4, f32[2,8,1,32,128]{4,1,3,2,0:T(8,128)S(1)} %get-tuple-element.960, s32[]{:T(128)} %get-tuple-element.938, ...), kind=kOutput, calls=%fused_computation.51.clone.1 | convolution fusion | flops 51474432 | bytes 2461700 | tf_op jit(solution)/shard_map/while/body/eval_jaxpr/bkrc,nc->nbkr/dot_general | solution.py:83
  163.1 2.2 fusion.275
  165.3 3.3 %fusion.273 = f32[32,128,128]{2,1,0:T(8,128)S(1)} fusion(s32[32,128]{1,0:T(8,128)S(1)} %dynamic-slice_bitcast_fusion.27, f32[1,384,128]{2,1,0:T(8,128)S(1)} %get-tuple-element.957), kind=kOutput, calls=%fused_computation.41.clone.1 | convolution fusion | flops 2417491968 | bytes 2310144 | tf_op jit(solution)/shard_map/while/body/eval_jaxpr/kre,bec->bkrc/dot_general | solution.py:80
  168.6 2.3 %fusion.274 = f32[32,128]{1,0:T(8,128)S(1)} fusion(f32[32,128,128]{2,1,0:T(8,128)S(1)} %fusion.273, f32[128,128]{1,0:T(8,128)S(1)} %dynamic-slice_bitcast_fusion.29, f32[32,128]{1,0:T(8,128)S(1)} %multiply_bitcast_fusion.4, f32[2,8,1,32,128]{4,1,3,2,0:T(8,128)S(1)} %get-tuple-element.960, s32[]{:T(128)} %get-tuple-element.938, ...), kind=kOutput, calls=%fused_computation.51.clone.1 | convolution fusion | flops 51474432 | bytes 2461700 | tf_op jit(solution)/shard_map/while/body/eval_jaxpr/bkrc,nc->nbkr/dot_general | solution.py:83
  171.1 2.2 fusion.275
  173.4 4.0 %collective-permute-start.7 = (f32[1,3,64]{2,1,0:T(4,128)S(1)}, f32[1,3,64]{2,1,0:T(4,128)S(1)}, u32[]{:S(2)}, u32[]{:S(2)}) collective-permute-start(f32[1,3,64]{2,1,0:T(4,128)S(1)} %get-tuple-element.546), channel_id=1, source_target_pairs={{1,0},{2,1},{3,2},{4,3},{5,4},{6,5},{7,6},{8,7},{9,8},{10,9},{11,1... | collective-permute-start | bytes 2312 | tf_op jit(solution)/shard_map/ppermute | solution.py:24
  177.3 1.2 collective-permute-done.6
  178.9 43.0 %all_gather.7 = f32[16,3,256]{2,1,0:T(4,128)S(1)} all-gather(f32[1,3,256]{2,1,0:T(4,128)S(1)} %fusion.116), channel_id=1, replica_groups=mesh['bead'=16,'space'=16] {'bead'}, dimensions={0}, use_global_device_ids=true | all-gather | bytes 52224 | tf_op jit(solution)/shard_map/all_gather | solution.py:249
  (114 shorter events, 17.9 us)
Async XLA Ops:
  0.0 52.6 %copy-start = (f32[2,128]{1,0:T(2,128)S(1)}, f32[2,128]{1,0:T(2,128)}, u32[]{:S(2)}) copy-start(f32[2,128]{1,0:T(2,128)} %param.27) | copy-start | bytes 3076
  46.7 7.8 %collective-permute-start = (f32[1,4,64]{2,1,0:T(4,128)S(1)}, f32[1,4,64]{2,1,0:T(4,128)S(1)}, u32[]{:S(2)}, u32[]{:S(2)}) collective-permute-start(f32[1,4,64]{2,1,0:T(4,128)S(1)} %get-tuple-element.552), channel_id=1, source_target_pairs={{0,1},{1,2},{2,3},{3,4},{4,5},{5,6},{6,7},{7,8},{8,9},{9,10},{10,1... | collective-permute-start | bytes 3080 | tf_op jit(solution)/shard_map/ppermute | solution.py:21
  46.7 7.8 %collective-permute-start.1 = (f32[1,4,64]{2,1,0:T(4,128)S(1)}, f32[1,4,64]{2,1,0:T(4,128)S(1)}, u32[]{:S(2)}, u32[]{:S(2)}) collective-permute-start(f32[1,4,64]{2,1,0:T(4,128)S(1)} %get-tuple-element.553), channel_id=1, source_target_pairs={{1,0},{2,1},{3,2},{4,3},{5,4},{6,5},{7,6},{8,7},{9,8},{10,9},{11,1... | collective-permute-start | bytes 3080 | tf_op jit(solution)/shard_map/ppermute | solution.py:24
  62.6 19.7 %copy-start.1 = (f32[2,128,128]{2,1,0:T(8,128)S(1)}, f32[2,128,128]{2,1,0:T(8,128)}, u32[]{:S(2)}) copy-start(f32[2,128,128]{2,1,0:T(8,128)} %param.30) | copy-start | bytes 393220
  62.6 20.6 %copy-start.3 = (s32[256]{0:T(256)S(1)}, s32[256]{0:T(256)}, u32[]{:S(2)}) copy-start(s32[256]{0:T(256)} %param.23) | copy-start | bytes 3076
  62.7 22.0 %copy-start.4 = (s32[128]{0:T(128)S(1)}, s32[128]{0:T(128)}, u32[]{:S(2)}) copy-start(s32[128]{0:T(128)} %param.26) | copy-start | bytes 1540
  82.6 0.6 copy-start.2
  85.0 5.5 %collective-permute-start.2 = (f32[1,64,128]{2,1,0:T(8,128)S(1)}, f32[1,64,128]{2,1,0:T(8,128)S(1)}, u32[]{:S(2)}, u32[]{:S(2)}) collective-permute-start(f32[1,64,128]{2,1,0:T(8,128)S(1)} %get-tuple-element.537), channel_id=1, source_target_pairs={{0,1},{1,2},{2,3},{3,4},{4,5},{5,6},{6,7},{7,8},{8,9},{9,10},{10,1... | collective-permute-start | bytes 98312 | tf_op jit(solution)/shard_map/ppermute | solution.py:21
  85.1 5.9 %collective-permute-start.3 = (f32[1,64,128]{2,1,0:T(8,128)S(1)}, f32[1,64,128]{2,1,0:T(8,128)S(1)}, u32[]{:S(2)}, u32[]{:S(2)}) collective-permute-start(f32[1,64,128]{2,1,0:T(8,128)S(1)} %get-tuple-element.538), channel_id=1, source_target_pairs={{1,0},{2,1},{3,2},{4,3},{5,4},{6,5},{7,6},{8,7},{9,8},{10,9},{11,1... | collective-permute-start | bytes 98312 | tf_op jit(solution)/shard_map/ppermute | solution.py:24
  91.7 20.9 %copy-start.5 = (f32[128]{0:T(128)S(1)}, f32[128]{0:T(128)}, u32[]{:S(2)}) copy-start(f32[128]{0:T(128)} %param.31) | copy-start | bytes 1540
  147.5 6.1 %collective-permute-start.4 = (f32[1,64,128]{1,2,0:T(8,128)S(1)}, f32[1,64,128]{1,2,0:T(8,128)S(1)}, u32[]{:S(2)}, u32[]{:S(2)}) collective-permute-start(f32[1,64,128]{1,2,0:T(8,128)S(1)} %get-tuple-element.535), channel_id=1, source_target_pairs={{0,1},{1,2},{2,3},{3,4},{4,5},{5,6},{6,7},{7,8},{8,9},{9,10},{10,1... | collective-permute-start | bytes 98312 | tf_op jit(solution)/shard_map/ppermute | solution.py:21
  147.8 5.8 %collective-permute-start.5 = (f32[1,64,128]{1,2,0:T(8,128)S(1)}, f32[1,64,128]{1,2,0:T(8,128)S(1)}, u32[]{:S(2)}, u32[]{:S(2)}) collective-permute-start(f32[1,64,128]{1,2,0:T(8,128)S(1)} %get-tuple-element.536), channel_id=1, source_target_pairs={{1,0},{2,1},{3,2},{4,3},{5,4},{6,5},{7,6},{8,7},{9,8},{10,9},{11,1... | collective-permute-start | bytes 98312 | tf_op jit(solution)/shard_map/ppermute | solution.py:24
  173.3 5.2 %collective-permute-start.6 = (f32[1,3,64]{2,1,0:T(4,128)S(1)}, f32[1,3,64]{2,1,0:T(4,128)S(1)}, u32[]{:S(2)}, u32[]{:S(2)}) collective-permute-start(f32[1,3,64]{2,1,0:T(4,128)S(1)} %get-tuple-element.545), channel_id=1, source_target_pairs={{0,1},{1,2},{2,3},{3,4},{4,5},{5,6},{6,7},{7,8},{8,9},{9,10},{10,1... | collective-permute-start | bytes 2312 | tf_op jit(solution)/shard_map/ppermute | solution.py:21
  173.4 5.3 %collective-permute-start.7 = (f32[1,3,64]{2,1,0:T(4,128)S(1)}, f32[1,3,64]{2,1,0:T(4,128)S(1)}, u32[]{:S(2)}, u32[]{:S(2)}) collective-permute-start(f32[1,3,64]{2,1,0:T(4,128)S(1)} %get-tuple-element.546), channel_id=1, source_target_pairs={{1,0},{2,1},{3,2},{4,3},{5,4},{6,5},{7,6},{8,7},{9,8},{10,9},{11,1... | collective-permute-start | bytes 2312 | tf_op jit(solution)/shard_map/ppermute | solution.py:24
where the time goes:
time: 226 us; the launch traced here: 223 us
  matrix products  104 us (46%)
  blocking collectives  85.8 us (38%)
  starting transfers between devices  16.5 us (7%)
  local copies, waits for them, and re-layouts  5.61 us (2%)
  waiting for transfers between devices  4.79 us (2%)
  other arithmetic  4.56 us (2%)
    all_gather x1, blocking collectives, on_device(): lax.all_gather(pull_reduced, 'bead', axis=0, tiled=True)  43 us
    all_gather x1, blocking collectives, on_device(): lax.all_gather(positions, 'bead', axis=0, tiled=True)  42.8 us
    ppermute x4, starting transfers between devices, with_halo(): lax.ppermute(lax.slice_in_dim(block, 0, width, axis=dim), axis, backward)  16.1 us
    dot_general x4, matrix products, block_message(): jnp.einsum('nbkr,nc->bkrc', radial_basis, radial_map, precision=exact_mode)  13.8 us
    dot_general x4, matrix products, block_message(): jnp.einsum('kre,bec->bkrc', chooser, lent_ext, precision=exact_mode)  13.3 us
    dot_general x4, matrix products, block_backward(): jnp.einsum('kre,bec->bkrc', chooser, lent_ext, precision=exact_mode)  13 us
    dot_general x4, matrix products, block_message(): jnp.einsum('bkrc,kr->brc', radial_w * near_rows, live_slots, precision=ex...  11.6 us
    dot_general x4, matrix products, block_backward(): jnp.einsum('bkrc,nc->nbkr', grad_radial, radial_map, precision=exact_mode)  9.4 us
  transfers between devices with their start and end apart: 8, of which 5 were waited for; matrix products, arithmetic and copies ran while one was open for 2% of the time, Pallas kernels for 0%

commit v1 on v0

--- a/solution.py
+++ b/solution.py
@@ -246,7 +246,9 @@
     return ratio * jnp.einsum(
         "kj,kcn->jcn",
         weights,
-        lax.all_gather(pull_reduced, "bead", axis=0, tiled=True),
+        jnp.concatenate(
+            lax.all_to_all(jnp.stack([pull_reduced] * lax.axis_size("bead")), "bead", 0, 0), axis=0
+        ),
         precision=exact_mode,
     )
 

time: 226 us -> 202 us (0.89)
  the two profiles are of different devices: /device:TPU:64 before, /device:TPU:25 now
where the time goes in v1:
time: 202 us; the launch traced here: 199 us
  matrix products  104 us (51%)
  blocking collectives  40.9 us (20%)
  waiting for transfers between devices  25.6 us (13%)
  starting transfers between devices  16.2 us (8%)
  local copies, waits for them, and re-layouts  6.29 us (3%)
  other arithmetic  4.54 us (2%)
    all_gather x1, blocking collectives, on_device(): lax.all_gather(positions, 'bead', axis=0, tiled=True)  40.9 us
    ppermute x4, waiting for transfers between devices, with_halo(): lax.ppermute(lax.slice_in_dim(block, 0, width, axis=dim), axis, backward)  14.7 us
    dot_general x4, matrix products, block_message(): jnp.einsum('nbkr,nc->bkrc', radial_basis, radial_map, precision=exact_mode)  13.8 us
    dot_general x4, matrix products, block_message(): jnp.einsum('kre,bec->bkrc', chooser, lent_ext, precision=exact_mode)  13.3 us
    dot_general x4, matrix products, block_backward(): jnp.einsum('kre,bec->bkrc', chooser, lent_ext, precision=exact_mode)  13 us
    dot_general x4, matrix products, block_message(): jnp.einsum('bkrc,kr->brc', radial_w * near_rows, live_slots, precision=ex...  11.6 us
    ppermute x4, starting transfers between devices, with_halo(): lax.ppermute(lax.slice_in_dim(block, block.shape[dim] - width, None, axis...  11.2 us
    dot_general x4, matrix products, block_backward(): jnp.einsum('bkrc,nc->nbkr', grad_radial, radial_map, precision=exact_mode)  9.4 us
  transfers between devices with their start and end apart: 9, of which 8 were waited for; matrix products, arithmetic and copies ran while one was open for 2% of the time, Pallas kernels for 0%

profile of v1, /device:TPU:25, one launch (start us, length us, event | category | flops | bytes accessed | tf_op | source)
XLA Modules:
  0.0 199.1 jit_solution(6911686071572154424)
XLA Ops:
  0.7 40.9 %all_gather.3 = f32[64,3,256]{2,1,0:T(4,128)S(1)} all-gather(f32[4,3,256]{2,1,0:T(4,128)S(1)} %copy.51), channel_id=1, replica_groups=mesh['bead'=16,'space'=16] {'bead'}, dimensions={0}, use_global_device_ids=true | all-gather | bytes 208896 | tf_op jit(solution)/shard_map/all_gather | solution.py:112
  44.7 8.1 %collective-permute-start = (f32[1,4,64]{2,1,0:T(4,128)S(1)}, f32[1,4,64]{2,1,0:T(4,128)S(1)}, u32[]{:S(2)}, u32[]{:S(2)}) collective-permute-start(f32[1,4,64]{2,1,0:T(4,128)S(1)} %get-tuple-element.595), channel_id=1, source_target_pairs={{0,1},{1,2},{2,3},{3,4},{4,5},{5,6},{6,7},{7,8},{8,9},{9,10},{10,1... | collective-permute-start | bytes 3080 | tf_op jit(solution)/shard_map/ppermute | solution.py:21
  56.7 1.2 collective-permute-done.1
  58.3 7.0 %while.58 = (s32[]{:T(128)}, f32[2,1,3,32,128]{4,2,3,1,0:T(4,128)S(1)}, s32[2,32,128]{2,1,0:T(8,128)S(1)}, f32[1,3,384]{2,1,0:T(4,128)S(1)}, s32[]{:T(128)}) while((s32[]{:T(128)}, f32[2,1,3,32,128]{4,2,3,1,0:T(4,128)S(1)}, s32[2,32,128]{2,1,0:T(8,128)S(1)}, f32[1,3,384]{2,1,0:T(4,128)S(1)}, s32[]{:T(128)}) %tuple.111), condition=%wide.region_1.2_spmd, body=%wide.region_0.1_spmd.sunk | while | flops 58195968 | bytes 120901 | solution.py:141
  58.4 3.5 %fusion.254 = f32[2,1,3,32,128]{4,2,3,1,0:T(4,128)S(1)} fusion(f32[2,1,3,32,128]{4,2,3,1,0:T(4,128)S(1)} %get-tuple-element.866, s32[]{:T(128)} %get-tuple-element.865, s32[32,128]{1,0:T(8,128)S(1)} %dynamic-slice_bitcast_fusion.22, f32[1,3,384]{2,1,0:T(4,128)S(1)} %get-tuple-element.873), kind=kOutput, calls=%fused_computation.4.clone.1 | convolution fusion | flops 58195968 | bytes 88068 | tf_op jit(solution)/shard_map/while/body/eval_jaxpr/kre,bce->bckr/dot_general | solution.py:139
  61.9 3.5 %fusion.254 = f32[2,1,3,32,128]{4,2,3,1,0:T(4,128)S(1)} fusion(f32[2,1,3,32,128]{4,2,3,1,0:T(4,128)S(1)} %get-tuple-element.866, s32[]{:T(128)} %get-tuple-element.865, s32[32,128]{1,0:T(8,128)S(1)} %dynamic-slice_bitcast_fusion.22, f32[1,3,384]{2,1,0:T(4,128)S(1)} %get-tuple-element.873), kind=kOutput, calls=%fused_computation.4.clone.1 | convolution fusion | flops 58195968 | bytes 88068 | tf_op jit(solution)/shard_map/while/body/eval_jaxpr/kre,bce->bckr/dot_general | solution.py:139
  66.1 19.7 %while.59 = (s32[]{:T(128)}, f32[2,1,128,128]{3,2,1,0:T(8,128)S(1)}, f32[2,32,128]{2,1,0:T(8,128)S(1)}, f32[2,8,1,32,128]{4,1,3,2,0:T(8,128)S(1)}, f32[8,128]{1,...) while((s32[]{:T(128)}, f32[2,1,128,128]{3,2,1,0:T(8,128)S(1)}, ...), condition=%wide.region_4.5_spmd, body=%wide.region_3.4_spmd.sunk | while | flops 2474655744 | bytes 9048165 | solution.py:179
  66.1 3.4 %fusion.260 = f32[32,128,128]{2,1,0:T(8,128)S(1)} fusion(f32[2,8,1,32,128]{4,1,3,2,0:T(8,128)S(1)} %get-tuple-element.894, s32[]{:T(128)} %get-tuple-element.883, f32[8,128]{1,0:T(8,128)S(1)} %get-tuple-element.895), kind=kOutput, calls=%fused_computation.15.clone.1 | convolution fusion | flops 50331648 | bytes 2232324 | tf_op jit(solution)/shard_map/while/body/eval_jaxpr/nbkr,nc->bkrc/dot_general | solution.py:67
  69.6 3.3 %fusion.261 = f32[32,128,128]{2,1,0:T(8,128)S(1)} fusion(f32[32,128,128]{2,1,0:T(8,128)S(1)} %fusion.260, s32[32,128]{1,0:T(8,128)S(1)} %dynamic-slice_bitcast_fusion.24, f32[1,384,128]{2,1,0:T(8,128)S(1)} %get-tuple-element.897), kind=kOutput, calls=%fused_computation.11.clone.1 | convolution fusion | flops 2418016256 | bytes 4407296 | tf_op jit(solution)/shard_map/while/body/eval_jaxpr/kre,bec->bkrc/dot_general | solution.py:69
  73.0 2.9 %fusion.262 = f32[128,1,128]{2,1,0:T(1,128)S(1)} fusion(f32[32,128,1]{0,2,1:T(1,128)S(1)} %copy.97, f32[32,128,128]{2,1,0:T(8,128)S(1)} %fusion.261), kind=kOutput, calls=%fused_computation.12.clone.1 | convolution fusion | flops 6291456 | bytes 2179072 | tf_op jit(solution)/shard_map/while/body/eval_jaxpr/bkrc,kr->brc/dot_general | solution.py:70
  76.0 3.4 %fusion.260 = f32[32,128,128]{2,1,0:T(8,128)S(1)} fusion(f32[2,8,1,32,128]{4,1,3,2,0:T(8,128)S(1)} %get-tuple-element.894, s32[]{:T(128)} %get-tuple-element.883, f32[8,128]{1,0:T(8,128)S(1)} %get-tuple-element.895), kind=kOutput, calls=%fused_computation.15.clone.1 | convolution fusion | flops 50331648 | bytes 2232324 | tf_op jit(solution)/shard_map/while/body/eval_jaxpr/nbkr,nc->bkrc/dot_general | solution.py:67
  79.4 3.3 %fusion.261 = f32[32,128,128]{2,1,0:T(8,128)S(1)} fusion(f32[32,128,128]{2,1,0:T(8,128)S(1)} %fusion.260, s32[32,128]{1,0:T(8,128)S(1)} %dynamic-slice_bitcast_fusion.24, f32[1,384,128]{2,1,0:T(8,128)S(1)} %get-tuple-element.897), kind=kOutput, calls=%fused_computation.11.clone.1 | convolution fusion | flops 2418016256 | bytes 4407296 | tf_op jit(solution)/shard_map/while/body/eval_jaxpr/kre,bec->bkrc/dot_general | solution.py:69
  82.9 2.9 %fusion.262 = f32[128,1,128]{2,1,0:T(1,128)S(1)} fusion(f32[32,128,1]{0,2,1:T(1,128)S(1)} %copy.97, f32[32,128,128]{2,1,0:T(8,128)S(1)} %fusion.261), kind=kOutput, calls=%fused_computation.12.clone.1 | convolution fusion | flops 6291456 | bytes 2179072 | tf_op jit(solution)/shard_map/while/body/eval_jaxpr/bkrc,kr->brc/dot_general | solution.py:70
  88.4 2.8 %collective-permute-start.2 = (f32[1,64,128]{2,1,0:T(8,128)S(1)}, f32[1,64,128]{2,1,0:T(8,128)S(1)}, u32[]{:S(2)}, u32[]{:S(2)}) collective-permute-start(f32[1,64,128]{2,1,0:T(8,128)S(1)} %get-tuple-element.580), channel_id=1, source_target_pairs={{0,1},{1,2},{2,3},{3,4},{4,5},{5,6},{6,7},{7,8},{8,9},{9,10},{10,1... | collective-permute-start | bytes 98312 | tf_op jit(solution)/shard_map/ppermute | solution.py:21
  92.2 4.9 %collective-permute-done.3 = f32[1,64,128]{2,1,0:T(8,128)S(1)} collective-permute-done((f32[1,64,128]{2,1,0:T(8,128)S(1)}, f32[1,64,128]{2,1,0:T(8,128)S(1)}, u32[]{:S(2)}, u32[]{:S(2)}) %collective-permute-start.3) | collective-permute-done | bytes 32800 | tf_op jit(solution)/shard_map/ppermute | solution.py:24
  97.8 20.9 %while.60 = (s32[]{:T(128)}, f32[2,1,128,128]{3,2,1,0:T(8,128)}, f32[2,32,128]{2,1,0:T(8,128)S(1)}, f32[2,8,1,32,128]{4,1,3,2,0:T(8,128)S(1)}, f32[8,128]{1,0:T(...) while((s32[]{:T(128)}, f32[2,1,128,128]{3,2,1,0:T(8,128)}, ...), condition=%wide.region_6.7_spmd, body=%wide.region_5.6_spmd.sunk | while | flops 2474655744 | bytes 9048673 | solution.py:179
  97.8 3.4 %fusion.268 = f32[32,128,128]{2,1,0:T(8,128)S(1)} fusion(f32[2,8,1,32,128]{4,1,3,2,0:T(8,128)S(1)} %get-tuple-element.918, s32[]{:T(128)} %get-tuple-element.907, f32[8,128]{1,0:T(8,128)S(1)} %get-tuple-element.919), kind=kOutput, calls=%fused_computation.31.clone.1 | convolution fusion | flops 50331648 | bytes 2232324 | tf_op jit(solution)/shard_map/while/body/eval_jaxpr/nbkr,nc->bkrc/dot_general | solution.py:67
  101.3 3.3 %fusion.269 = f32[32,128,128]{2,1,0:T(8,128)S(1)} fusion(f32[32,128,128]{2,1,0:T(8,128)S(1)} %fusion.268, s32[32,128]{1,0:T(8,128)S(1)} %dynamic-slice_bitcast_fusion.26, f32[1,384,128]{2,1,0:T(8,128)S(1)} %get-tuple-element.921), kind=kOutput, calls=%fused_computation.27.clone.1 | convolution fusion | flops 2418016256 | bytes 4407296 | tf_op jit(solution)/shard_map/while/body/eval_jaxpr/kre,bec->bkrc/dot_general | solution.py:69
  104.7 2.9 %fusion.270 = f32[128,1,128]{2,1,0:T(1,128)S(1)} fusion(f32[32,128,1]{0,2,1:T(1,128)S(1)} %copy.99, f32[32,128,128]{2,1,0:T(8,128)S(1)} %fusion.269), kind=kOutput, calls=%fused_computation.28.clone.1 | convolution fusion | flops 6291456 | bytes 2179072 | tf_op jit(solution)/shard_map/while/body/eval_jaxpr/bkrc,kr->brc/dot_general | solution.py:70
  108.3 3.4 %fusion.268 = f32[32,128,128]{2,1,0:T(8,128)S(1)} fusion(f32[2,8,1,32,128]{4,1,3,2,0:T(8,128)S(1)} %get-tuple-element.918, s32[]{:T(128)} %get-tuple-element.907, f32[8,128]{1,0:T(8,128)S(1)} %get-tuple-element.919), kind=kOutput, calls=%fused_computation.31.clone.1 | convolution fusion | flops 50331648 | bytes 2232324 | tf_op jit(solution)/shard_map/while/body/eval_jaxpr/nbkr,nc->bkrc/dot_general | solution.py:67
  111.7 3.3 %fusion.269 = f32[32,128,128]{2,1,0:T(8,128)S(1)} fusion(f32[32,128,128]{2,1,0:T(8,128)S(1)} %fusion.268, s32[32,128]{1,0:T(8,128)S(1)} %dynamic-slice_bitcast_fusion.26, f32[1,384,128]{2,1,0:T(8,128)S(1)} %get-tuple-element.921), kind=kOutput, calls=%fused_computation.27.clone.1 | convolution fusion | flops 2418016256 | bytes 4407296 | tf_op jit(solution)/shard_map/while/body/eval_jaxpr/kre,bec->bkrc/dot_general | solution.py:69
  115.2 2.9 %fusion.270 = f32[128,1,128]{2,1,0:T(1,128)S(1)} fusion(f32[32,128,1]{0,2,1:T(1,128)S(1)} %copy.99, f32[32,128,128]{2,1,0:T(8,128)S(1)} %fusion.269), kind=kOutput, calls=%fused_computation.28.clone.1 | convolution fusion | flops 6291456 | bytes 2179072 | tf_op jit(solution)/shard_map/while/body/eval_jaxpr/bkrc,kr->brc/dot_general | solution.py:70
  118.7 1.2 multiply_multiply_fusion
  120.2 32.4 %while.62 = (s32[]{:T(128)}, f32[1,384,128]{1,2,0:T(8,128)}, f32[1,3,384]{2,1,0:T(4,128)S(1)}, f32[2,1,3,128]{3,2,1,0:T(4,128)S(1)}, f32[2,32,128]{2,1,0:T(8,128...) while((s32[]{:T(128)}, f32[1,384,128]{1,2,0:T(8,128)}, ...), condition=%wide.region_10.11_spmd.clone, body=%wide.region_7.10_spmd.clone.sunk | while | flops 4996204544 | bytes 10068156 | solution.py:219
  120.4 3.4 %fusion.286 = f32[32,128,128]{2,1,0:T(8,128)S(1)} fusion(f32[2,8,1,32,128]{4,1,3,2,0:T(8,128)S(1)} %get-tuple-element.959, s32[]{:T(128)} %get-tuple-element.938, f32[8,128]{1,0:T(8,128)S(1)} %get-tuple-element.960), kind=kOutput, calls=%fused_computation.99.clone.1 | convolution fusion | flops 50331648 | bytes 2232324 | tf_op jit(solution)/shard_map/while/body/eval_jaxpr/nbkr,nc->bkrc/dot_general | solution.py:78
  123.9 4.2 %fusion.287 = f32[1,384,128]{1,2,0:T(8,128)} fusion(s32[32,128]{1,0:T(8,128)S(1)} %dynamic-slice_bitcast_fusion.30, f32[32,128,128]{2,1,0:T(8,128)S(1)} %fusion.286, f32[128,128]{1,0:T(8,128)S(1)} %dynamic-slice_bitcast_fusion.31, f32[32,128]{1,0:T(8,128)S(1)} %multiply_bitcast_fusion.5, f32[1,384,128]{1,2,0:T(8,128)} %get-tuple-element.939, ...), kind=kOutput, calls=%fused_computation.87.clone.1 | convolution fusion | flops 2418638848 | bytes 2588673 | tf_op jit(solution)/shard_map/while/body/eval_jaxpr/kre,bkrc->bec/dot_general | solution.py:91
  128.1 3.2 %fusion.288 = f32[32,128,128]{2,1,0:T(8,128)S(1)} fusion(s32[32,128]{1,0:T(8,128)S(1)} %dynamic-slice_bitcast_fusion.30, f32[1,384,128]{2,1,0:T(8,128)S(1)} %get-tuple-element.962), kind=kOutput, calls=%fused_computation.75.clone.1 | convolution fusion | flops 2417491968 | bytes 2310144 | tf_op jit(solution)/shard_map/while/body/eval_jaxpr/kre,bec->bkrc/dot_general | solution.py:80
  131.4 2.4 %fusion.289 = f32[32,128]{1,0:T(8,128)S(1)} fusion(f32[32,128,128]{2,1,0:T(8,128)S(1)} %fusion.288, f32[128,128]{1,0:T(8,128)S(1)} %dynamic-slice_bitcast_fusion.31, f32[32,128]{1,0:T(8,128)S(1)} %multiply_bitcast_fusion.5, f32[2,8,1,32,128]{4,1,3,2,0:T(8,128)S(1)} %get-tuple-element.963, s32[]{:T(128)} %get-tuple-element.938, ...), kind=kOutput, calls=%fused_computation.91.clone.1 | convolution fusion | flops 51474432 | bytes 2461700 | tf_op jit(solution)/shard_map/while/body/eval_jaxpr/bkrc,nc->nbkr/dot_general | solution.py:83
  133.8 2.2 %fusion.290 = f32[1,3,384]{2,1,0:T(4,128)S(1)} fusion(s32[32,128]{1,0:T(8,128)S(1)} %dynamic-slice_bitcast_fusion.30, f32[2,1,3,32,128]{4,2,3,1,0:T(4,128)S(1)} %get-tuple-element.964, s32[]{:T(128)} %get-tuple-element.938, f32[32,128]{1,0:T(8,128)S(1)} %dynamic-slice_bitcast_fusion.32, f32[32,128]{1,0:T(8,128)S(1)} %broadcast_multiply_fusion.5, ...), kind=kOutput, calls=%fused_computation.93.clone.1 | convolution fusion | flops 58222848 | bytes 125445 | tf_op jit(solution)/shard_map/while/body/eval_jaxpr/kre,bckr->bce/dot_general | solution.py:86
  136.1 3.4 %fusion.286 = f32[32,128,128]{2,1,0:T(8,128)S(1)} fusion(f32[2,8,1,32,128]{4,1,3,2,0:T(8,128)S(1)} %get-tuple-element.959, s32[]{:T(128)} %get-tuple-element.938, f32[8,128]{1,0:T(8,128)S(1)} %get-tuple-element.960), kind=kOutput, calls=%fused_computation.99.clone.1 | convolution fusion | flops 50331648 | bytes 2232324 | tf_op jit(solution)/shard_map/while/body/eval_jaxpr/nbkr,nc->bkrc/dot_general | solution.py:78
  139.6 5.1 %fusion.287 = f32[1,384,128]{1,2,0:T(8,128)} fusion(s32[32,128]{1,0:T(8,128)S(1)} %dynamic-slice_bitcast_fusion.30, f32[32,128,128]{2,1,0:T(8,128)S(1)} %fusion.286, f32[128,128]{1,0:T(8,128)S(1)} %dynamic-slice_bitcast_fusion.31, f32[32,128]{1,0:T(8,128)S(1)} %multiply_bitcast_fusion.5, f32[1,384,128]{1,2,0:T(8,128)} %get-tuple-element.939, ...), kind=kOutput, calls=%fused_computation.87.clone.1 | convolution fusion | flops 2418638848 | bytes 2588673 | tf_op jit(solution)/shard_map/while/body/eval_jaxpr/kre,bkrc->bec/dot_general | solution.py:91
  144.7 3.2 %fusion.288 = f32[32,128,128]{2,1,0:T(8,128)S(1)} fusion(s32[32,128]{1,0:T(8,128)S(1)} %dynamic-slice_bitcast_fusion.30, f32[1,384,128]{2,1,0:T(8,128)S(1)} %get-tuple-element.962), kind=kOutput, calls=%fused_computation.75.clone.1 | convolution fusion | flops 2417491968 | bytes 2310144 | tf_op jit(solution)/shard_map/while/body/eval_jaxpr/kre,bec->bkrc/dot_general | solution.py:80
  147.9 2.4 %fusion.289 = f32[32,128]{1,0:T(8,128)S(1)} fusion(f32[32,128,128]{2,1,0:T(8,128)S(1)} %fusion.288, f32[128,128]{1,0:T(8,128)S(1)} %dynamic-slice_bitcast_fusion.31, f32[32,128]{1,0:T(8,128)S(1)} %multiply_bitcast_fusion.5, f32[2,8,1,32,128]{4,1,3,2,0:T(8,128)S(1)} %get-tuple-element.963, s32[]{:T(128)} %get-tuple-element.938, ...), kind=kOutput, calls=%fused_computation.91.clone.1 | convolution fusion | flops 51474432 | bytes 2461700 | tf_op jit(solution)/shard_map/while/body/eval_jaxpr/bkrc,nc->nbkr/dot_general | solution.py:83
  150.3 2.2 %fusion.290 = f32[1,3,384]{2,1,0:T(4,128)S(1)} fusion(s32[32,128]{1,0:T(8,128)S(1)} %dynamic-slice_bitcast_fusion.30, f32[2,1,3,32,128]{4,2,3,1,0:T(4,128)S(1)} %get-tuple-element.964, s32[]{:T(128)} %get-tuple-element.938, f32[32,128]{1,0:T(8,128)S(1)} %dynamic-slice_bitcast_fusion.32, f32[32,128]{1,0:T(8,128)S(1)} %broadcast_multiply_fusion.5, ...), kind=kOutput, calls=%fused_computation.93.clone.1 | convolution fusion | flops 58222848 | bytes 125445 | tf_op jit(solution)/shard_map/while/body/eval_jaxpr/kre,bckr->bce/dot_general | solution.py:86
  155.2 4.6 %collective-permute-done.5 = f32[1,64,128]{1,2,0:T(8,128)S(1)} collective-permute-done((f32[1,64,128]{1,2,0:T(8,128)S(1)}, f32[1,64,128]{1,2,0:T(8,128)S(1)}, u32[]{:S(2)}, u32[]{:S(2)}) %collective-permute-start.5) | collective-permute-done | bytes 32800 | tf_op jit(solution)/shard_map/ppermute | solution.py:24
  159.8 1.2 fusion.114
  161.0 1.3 fusion.112
  162.3 1.1 convolution_bitcast_fusion.1
  163.5 16.0 %while.61 = (s32[]{:T(128)}, f32[1,3,384]{2,1,0:T(4,128)S(1)}, f32[2,1,3,128]{3,2,1,0:T(4,128)S(1)}, f32[2,32,128]{2,1,0:T(8,128)S(1)}, f32[2,1,128,128]{3,2,1,0...) while((s32[]{:T(128)}, f32[1,3,384]{2,1,0:T(4,128)S(1)}, ...), condition=%wide.region_14.15_spmd, body=%wide.region_11.14_spmd.sunk | while | flops 2527233024 | bytes 5247133 | solution.py:219
  163.5 3.3 %fusion.275 = f32[32,128,128]{2,1,0:T(8,128)S(1)} fusion(s32[32,128]{1,0:T(8,128)S(1)} %dynamic-slice_bitcast_fusion.27, f32[1,384,128]{2,1,0:T(8,128)S(1)} %get-tuple-element.1000), kind=kOutput, calls=%fused_computation.41.clone.1 | convolution fusion | flops 2417491968 | bytes 2310144 | tf_op jit(solution)/shard_map/while/body/eval_jaxpr/kre,bec->bkrc/dot_general | solution.py:80
  166.8 2.3 %fusion.276 = f32[32,128]{1,0:T(8,128)S(1)} fusion(f32[32,128,128]{2,1,0:T(8,128)S(1)} %fusion.275, f32[128,128]{1,0:T(8,128)S(1)} %dynamic-slice_bitcast_fusion.29, f32[32,128]{1,0:T(8,128)S(1)} %multiply_bitcast_fusion.4, f32[2,8,1,32,128]{4,1,3,2,0:T(8,128)S(1)} %get-tuple-element.1003, s32[]{:T(128)} %get-tuple-element.981, ...), kind=kOutput, calls=%fused_computation.51.clone.1 | convolution fusion | flops 51474432 | bytes 2461700 | tf_op jit(solution)/shard_map/while/body/eval_jaxpr/bkrc,nc->nbkr/dot_general | solution.py:83
  169.3 2.2 %fusion.277 = f32[1,3,384]{2,1,0:T(4,128)S(1)} fusion(f32[1,3,384]{2,1,0:T(4,128)S(1)} %get-tuple-element.982, s32[32,128]{1,0:T(8,128)S(1)} %dynamic-slice_bitcast_fusion.27, f32[2,1,3,32,128]{4,2,3,1,0:T(4,128)S(1)} %get-tuple-element.1004, s32[]{:T(128)} %get-tuple-element.981, f32[32,128]{1,0:T(8,128)S(1)} %dynamic-slice_bitcast_fusion.28, ...), kind=kOutput, calls=%fused_computation.53.clone.1 | convolution fusion | flops 58221696 | bytes 125444 | tf_op jit(solution)/shard_map/while/body/eval_jaxpr/kre,bckr->bce/dot_general | solution.py:86
  171.5 3.3 %fusion.275 = f32[32,128,128]{2,1,0:T(8,128)S(1)} fusion(s32[32,128]{1,0:T(8,128)S(1)} %dynamic-slice_bitcast_fusion.27, f32[1,384,128]{2,1,0:T(8,128)S(1)} %get-tuple-element.1000), kind=kOutput, calls=%fused_computation.41.clone.1 | convolution fusion | flops 2417491968 | bytes 2310144 | tf_op jit(solution)/shard_map/while/body/eval_jaxpr/kre,bec->bkrc/dot_general | solution.py:80
  174.8 2.3 %fusion.276 = f32[32,128]{1,0:T(8,128)S(1)} fusion(f32[32,128,128]{2,1,0:T(8,128)S(1)} %fusion.275, f32[128,128]{1,0:T(8,128)S(1)} %dynamic-slice_bitcast_fusion.29, f32[32,128]{1,0:T(8,128)S(1)} %multiply_bitcast_fusion.4, f32[2,8,1,32,128]{4,1,3,2,0:T(8,128)S(1)} %get-tuple-element.1003, s32[]{:T(128)} %get-tuple-element.981, ...), kind=kOutput, calls=%fused_computation.51.clone.1 | convolution fusion | flops 51474432 | bytes 2461700 | tf_op jit(solution)/shard_map/while/body/eval_jaxpr/bkrc,nc->nbkr/dot_general | solution.py:83
  177.2 2.2 %fusion.277 = f32[1,3,384]{2,1,0:T(4,128)S(1)} fusion(f32[1,3,384]{2,1,0:T(4,128)S(1)} %get-tuple-element.982, s32[32,128]{1,0:T(8,128)S(1)} %dynamic-slice_bitcast_fusion.27, f32[2,1,3,32,128]{4,2,3,1,0:T(4,128)S(1)} %get-tuple-element.1004, s32[]{:T(128)} %get-tuple-element.981, f32[32,128]{1,0:T(8,128)S(1)} %dynamic-slice_bitcast_fusion.28, ...), kind=kOutput, calls=%fused_computation.53.clone.1 | convolution fusion | flops 58221696 | bytes 125444 | tf_op jit(solution)/shard_map/while/body/eval_jaxpr/kre,bckr->bce/dot_general | solution.py:86
  180.7 4.0 %collective-permute-done.7 = f32[1,3,64]{2,1,0:T(4,128)S(1)} collective-permute-done((f32[1,3,64]{2,1,0:T(4,128)S(1)}, f32[1,3,64]{2,1,0:T(4,128)S(1)}, u32[]{:S(2)}, u32[]{:S(2)}) %collective-permute-start.7) | collective-permute-done | bytes 800 | tf_op jit(solution)/shard_map/ppermute | solution.py:24
  185.6 3.5 %all-to-all-start = ((f32[16,1,3,256]{3,1,2,0:T(1,128)}), f32[16,1,3,256]{3,1,2,0:T(1,128)S(1)}, u32[]{:S(2)}, u32[]{:S(2)}) async-start(f32[16,1,3,256]{3,1,2,0:T(1,128)} %stack.2), calls=%async_computation | async-start | bytes 98304 | tf_op jit(solution)/shard_map/all_to_all | solution.py:250
  189.1 8.9 %all-to-all-done = f32[16,1,3,256]{3,1,2,0:T(1,128)S(1)} async-done(((f32[16,1,3,256]{3,1,2,0:T(1,128)}), f32[16,1,3,256]{3,1,2,0:T(1,128)S(1)}, u32[]{:S(2)}, u32[]{:S(2)}) %all-to-all-start) | async-done | bytes 49184 | tf_op jit(solution)/shard_map/all_to_all | solution.py:250
  (116 shorter events, 21.2 us)
Async XLA Ops:
  0.0 54.9 %copy-start = (f32[2,128]{1,0:T(2,128)S(1)}, f32[2,128]{1,0:T(2,128)}, u32[]{:S(2)}) copy-start(f32[2,128]{1,0:T(2,128)} %param.27) | copy-start | bytes 3076
  44.7 12.0 %collective-permute-start = (f32[1,4,64]{2,1,0:T(4,128)S(1)}, f32[1,4,64]{2,1,0:T(4,128)S(1)}, u32[]{:S(2)}, u32[]{:S(2)}) collective-permute-start(f32[1,4,64]{2,1,0:T(4,128)S(1)} %get-tuple-element.595), channel_id=1, source_target_pairs={{0,1},{1,2},{2,3},{3,4},{4,5},{5,6},{6,7},{7,8},{8,9},{9,10},{10,1... | collective-permute-start | bytes 3080 | tf_op jit(solution)/shard_map/ppermute | solution.py:21
  52.8 5.1 %collective-permute-start.1 = (f32[1,4,64]{2,1,0:T(4,128)S(1)}, f32[1,4,64]{2,1,0:T(4,128)S(1)}, u32[]{:S(2)}, u32[]{:S(2)}) collective-permute-start(f32[1,4,64]{2,1,0:T(4,128)S(1)} %get-tuple-element.596), channel_id=1, source_target_pairs={{1,0},{2,1},{3,2},{4,3},{5,4},{6,5},{7,6},{8,7},{9,8},{10,9},{11,1... | collective-permute-start | bytes 3080 | tf_op jit(solution)/shard_map/ppermute | solution.py:24
  66.1 19.7 %copy-start.1 = (f32[2,128,128]{2,1,0:T(8,128)S(1)}, f32[2,128,128]{2,1,0:T(8,128)}, u32[]{:S(2)}) copy-start(f32[2,128,128]{2,1,0:T(8,128)} %param.30) | copy-start | bytes 393220
  66.1 20.7 %copy-start.3 = (s32[256]{0:T(256)S(1)}, s32[256]{0:T(256)}, u32[]{:S(2)}) copy-start(s32[256]{0:T(256)} %param.23) | copy-start | bytes 3076
  66.1 22.1 %copy-start.4 = (s32[128]{0:T(128)S(1)}, s32[128]{0:T(128)}, u32[]{:S(2)}) copy-start(s32[128]{0:T(128)} %param.26) | copy-start | bytes 1540
  86.1 0.7 copy-start.2
  88.4 3.8 %collective-permute-start.2 = (f32[1,64,128]{2,1,0:T(8,128)S(1)}, f32[1,64,128]{2,1,0:T(8,128)S(1)}, u32[]{:S(2)}, u32[]{:S(2)}) collective-permute-start(f32[1,64,128]{2,1,0:T(8,128)S(1)} %get-tuple-element.580), channel_id=1, source_target_pairs={{0,1},{1,2},{2,3},{3,4},{4,5},{5,6},{6,7},{7,8},{8,9},{9,10},{10,1... | collective-permute-start | bytes 98312 | tf_op jit(solution)/shard_map/ppermute | solution.py:21
  91.2 6.0 %collective-permute-start.3 = (f32[1,64,128]{2,1,0:T(8,128)S(1)}, f32[1,64,128]{2,1,0:T(8,128)S(1)}, u32[]{:S(2)}, u32[]{:S(2)}) collective-permute-start(f32[1,64,128]{2,1,0:T(8,128)S(1)} %get-tuple-element.581), channel_id=1, source_target_pairs={{1,0},{2,1},{3,2},{4,3},{5,4},{6,5},{7,6},{8,7},{9,8},{10,9},{11,1... | collective-permute-start | bytes 98312 | tf_op jit(solution)/shard_map/ppermute | solution.py:24
  97.8 20.9 %copy-start.5 = (f32[128]{0:T(128)S(1)}, f32[128]{0:T(128)}, u32[]{:S(2)}) copy-start(f32[128]{0:T(128)} %param.31) | copy-start | bytes 1540
  153.6 1.6 collective-permute-start.4
  153.9 5.9 %collective-permute-start.5 = (f32[1,64,128]{1,2,0:T(8,128)S(1)}, f32[1,64,128]{1,2,0:T(8,128)S(1)}, u32[]{:S(2)}, u32[]{:S(2)}) collective-permute-start(f32[1,64,128]{1,2,0:T(8,128)S(1)} %get-tuple-element.579), channel_id=1, source_target_pairs={{1,0},{2,1},{3,2},{4,3},{5,4},{6,5},{7,6},{8,7},{9,8},{10,9},{11,1... | collective-permute-start | bytes 98312 | tf_op jit(solution)/shard_map/ppermute | solution.py:24
  179.5 1.2 collective-permute-start.6
  179.6 5.2 %collective-permute-start.7 = (f32[1,3,64]{2,1,0:T(4,128)S(1)}, f32[1,3,64]{2,1,0:T(4,128)S(1)}, u32[]{:S(2)}, u32[]{:S(2)}) collective-permute-start(f32[1,3,64]{2,1,0:T(4,128)S(1)} %get-tuple-element.589), channel_id=1, source_target_pairs={{1,0},{2,1},{3,2},{4,3},{5,4},{6,5},{7,6},{8,7},{9,8},{10,9},{11,1... | collective-permute-start | bytes 2312 | tf_op jit(solution)/shard_map/ppermute | solution.py:24
  185.6 12.4 %all-to-all-start = ((f32[16,1,3,256]{3,1,2,0:T(1,128)}), f32[16,1,3,256]{3,1,2,0:T(1,128)S(1)}, u32[]{:S(2)}, u32[]{:S(2)}) async-start(f32[16,1,3,256]{3,1,2,0:T(1,128)} %stack.2), calls=%async_computation | async-start | bytes 98304 | tf_op jit(solution)/shard_map/all_to_all | solution.py:250
